TPU v7x, 256 devices: a whole 4x4x8 slice. The times are simulated.
256 devices in a mesh: row: 8 (over z), col: 32 (over y, x, core).
Axes of the slice: x: 4, y: 4, z: 8, core: 2. Of those that a mesh axis runs over, the one named last changes fastest.
Arguments:
- factor: bfloat16 [131072, 5, 1024], P('col', None, 'row'), may hold values from -0.0625 to 0.0625
- diag_inverse: bfloat16 [5, 1024, 1024], P(None, 'row'), may hold values from -1 to 2
- right_side: float32 [16, 128, 1024], P(None, 'col', 'row'), may hold values from -6 to 6
- tile_order: int32 [128], replicated, may hold values from 0 to 127, each once
- live_segments: int32 [16], replicated, may hold values from 2 to 5
Outputs:
- result: float32 [16, 128, 1024], P(None, 'col', 'row')
Inputs may be any that keep to these rules, and one draw needn't show every extreme that they name: `tile_order`: each of 0 to 127 appears once.
All inputs are finite; a program needn't handle non-finite values.
Results may differ from a plain program's by a relative error of at most 0.0019.
Values may be sent and summed in bfloat16 or wider, within the bound.
No kernel may reach another device: no remote copies, remote signals or barrier semaphores. Data moves between devices by JAX's collectives and lax.ppermute only.
A program may use at most 64 MiB of HBM per device.

v0:
```python
import functools

import jax
import jax.numpy as jnp
from jax import lax
from jax.experimental import pallas as pl
from jax.experimental.pallas import tpu as pltpu
from jax.sharding import PartitionSpec as P


NT = (((1,), (1,)), ((), ()))
F32 = jnp.float32
BF16 = jnp.bfloat16
CHIP, PLACE, MINE = 2, 3, 8


def to_all(array, axis, peers, groups=None):
    copies = jnp.broadcast_to(array[None], (peers, *array.shape))
    return lax.all_to_all(copies, axis, 0, 0, axis_index_groups=groups, tiled=True)


def from_mask(array, mask):
    size = lax.axis_size("col")
    return lax.ppermute(array, "col", [(i, i ^ mask) for i in range(size)])


def levels(size):
    bits = size.bit_length() - 1
    return [(low, min(2, bits - low)) for low in range(1, bits, 2)][::-1]


def moved_by_mask(array, parts):
    for (low, bits), part in zip(levels(lax.axis_size("col")), parts, strict=True):
        branches = [lambda value: value]
        for step in range(1, 1 << bits):
            branches.append(functools.partial(from_mask, mask=step << low))
        array = lax.switch(part, branches, array)
    return array


def window_kernel(at_ref, *refs):
    count = len(refs) // 2
    for rows_ref, out_ref in zip(refs[:count], refs[count:], strict=True):
        out_ref[...] = rows_ref[...]


def window_rows(at, factor, diag_inverse):
    section_count, width, tile_width = diag_inverse.shape

    def spec(section, index_map):
        return pl.BlockSpec((section, tile_width, width), index_map)

    later = range(1, section_count)
    return pl.pallas_call(
        window_kernel,
        out_shape=[jax.ShapeDtypeStruct((t, tile_width, width), factor.dtype) for t in later]
        + [jax.ShapeDtypeStruct(diag_inverse.shape, diag_inverse.dtype)],
        grid_spec=pltpu.PrefetchScalarGridSpec(
            num_scalar_prefetch=1,
            grid=(1,),
            in_specs=[spec(t, lambda i, at, t=t: (0, at[PLACE + t], 0)) for t in later]
            + [pl.BlockSpec(diag_inverse.shape, lambda i, at: (0, 0, 0))],
            out_specs=[spec(t, lambda i, at: (0, 0, 0)) for t in later]
            + [pl.BlockSpec(diag_inverse.shape, lambda i, at: (0, 0, 0))],
        ),
        compiler_params=pltpu.CompilerParams(vmem_limit_bytes=60 << 20),
        cost_estimate=pl.CostEstimate(flops=0, bytes_accessed=7 << 20, transcendentals=0),
    )(at, *[factor for _ in later], diag_inverse)


def partial_kernel(section, at_ref, sent_ref, own_ref, other_ref, own_side, other_side, out_ref):
    me, core = at_ref[0], at_ref[1]
    peers, half, _ = out_ref.shape
    width = own_side.shape[2]
    columns = pl.ds(pl.multiple_of(me * width, width), width)

    def write(rows_ref, side_ref):
        total = lax.dot_general(sent_ref[0], rows_ref[0], NT, preferred_element_type=F32)
        for before in range(1, section):
            total = total + lax.dot_general(
                sent_ref[before], rows_ref[before], NT, preferred_element_type=F32
            )
        value = -jnp.where(core == 0, total[:half], total[half:])
        side = jnp.where(core == 0, side_ref[0, :half], side_ref[0, half:])
        for peer in range(peers):
            out_ref[peer] = value
            out_ref[peer, :, columns] = out_ref[peer, :, columns] + side

    mine = at_ref[MINE + section]

    @pl.when(mine == 1)
    def _():
        write(own_ref, own_side)

    @pl.when(mine != 1)
    def _():
        write(other_ref, other_side)


def partial_half(section, at, sent, own_rows, other_rows, own_sides, other_sides, peers):
    _, rhs_count, width = sent.shape
    tile_width = own_rows.shape[1]
    half = rhs_count // 2
    rows = pl.BlockSpec((section, tile_width, width), lambda i, at: (0, 0, 0))
    side = pl.BlockSpec((1, rhs_count, width), lambda i, at: (section, 0, 0))
    return pl.pallas_call(
        functools.partial(partial_kernel, section),
        out_shape=jax.ShapeDtypeStruct((peers, half, tile_width), F32),
        grid_spec=pltpu.PrefetchScalarGridSpec(
            num_scalar_prefetch=1,
            grid=(1,),
            in_specs=[
                pl.BlockSpec((section, rhs_count, width), lambda i, at: (0, 0, 0)),
                rows,
                rows,
                side,
                side,
            ],
            out_specs=pl.BlockSpec((peers, half, tile_width), lambda i, at: (0, 0, 0)),
        ),
        compiler_params=pltpu.CompilerParams(vmem_limit_bytes=8 << 20),
        cost_estimate=pl.CostEstimate(
            flops=2 * section * rhs_count * width * tile_width,
            bytes_accessed=4 * section * width * tile_width,
            transcendentals=0,
        ),
    )(at, sent, own_rows, other_rows, own_sides, other_sides)


def trailing_kernel(at_ref, sent_ref, rows_ref, out_ref):
    total = lax.dot_general(sent_ref[0, 0], rows_ref[0], NT, preferred_element_type=F32)
    for before in range(1, rows_ref.shape[0]):
        total = total + lax.dot_general(
            sent_ref[0, before], rows_ref[before], NT, preferred_element_type=F32
        )
    width = out_ref.shape[3]
    for peer in range(out_ref.shape[0]):
        out_ref[peer, 0] = total[:, peer * width : (peer + 1) * width]


def trailing(at, sent, factor, tile_width, peers):
    _, count, rhs_count, width = sent.shape
    tiles = factor.shape[1] // tile_width
    return pl.pallas_call(
        trailing_kernel,
        out_shape=jax.ShapeDtypeStruct((peers, tiles, rhs_count, width), F32),
        grid_spec=pltpu.PrefetchScalarGridSpec(
            num_scalar_prefetch=1,
            grid=(tiles,),
            in_specs=[
                pl.BlockSpec((1, count, rhs_count, width), lambda i, at: (at[CHIP], 0, 0, 0)),
                pl.BlockSpec((count, tile_width, width), lambda i, at: (0, i, 0)),
            ],
            out_specs=pl.BlockSpec((peers, 1, rhs_count, width), lambda i, at: (0, i, 0, 0)),
        ),
        compiler_params=pltpu.CompilerParams(vmem_limit_bytes=60 << 20),
        cost_estimate=pl.CostEstimate(
            flops=2 * count * rhs_count * width * tile_width * tiles,
            bytes_accessed=2 * count * width * tile_width * tiles,
            transcendentals=0,
        ),
    )(at, sent, factor)


def per_device(factor, diag_inverse, right_side, tile_order, live_segments):
    section_count, slice_width, tile_width = diag_inverse.shape
    rhs_count, rows_dev, _ = right_side.shape
    half = rhs_count // 2
    peers = tile_width // slice_width
    cols = lax.axis_size("col")
    my_col, me = lax.axis_index("col"), lax.axis_index("row")
    core = my_col & 1
    factor = jnp.transpose(factor, (1, 0, 2))
    slots = tile_order[:section_count]
    owner = lax.div(slots, jnp.int32(rows_dev))
    place = lax.rem(slots, jnp.int32(rows_dev))
    local = jnp.arange(rows_dev, dtype=jnp.int32)
    order = jnp.arange(section_count, dtype=jnp.int32)
    here = place[:, None] == local[None, :]
    sides = jnp.where(here[:, None, :, None], right_side[None], 0.0).sum(axis=2)
    mine = owner == my_col

    def own_half(array):
        return jnp.where(core == 0, array[:half], array[half:])

    other_sides = from_mask(sides, 1)
    share = own_half(jnp.where(mine[0], sides[0], other_sides[0]))
    arrived = to_all(share, "row", peers)

    chip = lax.shift_right_logical(owner[-1], jnp.int32(1))
    head = jnp.stack([me, core, chip])
    at = jnp.concatenate([head, place, mine.astype(jnp.int32)]).astype(jnp.int32)
    *own_rows, inverses = window_rows(at, factor, diag_inverse)
    other_rows = [from_mask(rows, 1) for rows in own_rows]
    masks = owner[1:] ^ owner[:-1]
    parts = [
        [
            lax.shift_right_logical(masks[section], jnp.int32(low)) & ((1 << bits) - 1)
            for low, bits in levels(cols)
        ]
        for section in range(section_count - 1)
    ]
    live = order[:, None] < live_segments[None, :]
    taken = (here & mine[:, None])[:, None, :] & live[:, :, None]
    done = taken.any(axis=0)[:, :, None]
    first = (arrived, parts, at, live, taken, done, sides, other_sides, own_rows, other_rows, inverses)
    arrived, parts, at, live, taken, done, sides, other_sides, own_rows, other_rows, inverses = (
        lax.optimization_barrier(first)
    )

    remaining = jnp.moveaxis(arrived, 0, 1).reshape(half, tile_width)
    history = None
    result = jnp.zeros_like(right_side)
    for section in range(section_count):
        if section:
            copies = partial_half(
                section,
                at,
                history,
                own_rows[section - 1],
                other_rows[section - 1],
                sides,
                other_sides,
                peers,
            )
            copies, history, result = lax.optimization_barrier((copies, history, result))
            remaining = lax.all_to_all(copies, "row", 0, 0, tiled=True).sum(axis=0)
        solved = lax.dot_general(
            remaining,
            inverses[section].astype(F32),
            NT,
            precision=lax.Precision.HIGHEST,
            preferred_element_type=F32,
        )
        other = from_mask(solved, 1)
        solved = jnp.where(
            core == 0, jnp.concatenate([solved, other]), jnp.concatenate([other, solved])
        )
        result = jnp.where(taken[section][..., None], solved[:, None, :], result)
        sent = jnp.where(live[section][:, None], solved, 0.0).astype(BF16)[None]
        history = sent if history is None else jnp.concatenate([history, sent])
        if section < section_count - 1:
            history, result = lax.optimization_barrier((history, result))
            history = moved_by_mask(history, parts[section])
    history, result = lax.optimization_barrier((history, result))
    planes = [list(range(first, cols, 2)) for first in range(2)]
    everywhere = to_all(history, "col", cols // 2, planes)
    pieces = trailing(at, everywhere, factor, tile_width, peers)
    total = lax.all_to_all(pieces, "row", 0, 0, tiled=True).sum(axis=0)
    updated = right_side - jnp.moveaxis(total, 0, 1)
    return jnp.where(done, result, updated)


def solution(mesh):
    return jax.shard_map(
        per_device,
        mesh=mesh,
        in_specs=(P("col", None, "row"), P(None, "row", None), P(None, "col", "row"), P(), P()),
        out_specs=P(None, "col", "row"),
        check_vma=False,
    )
```

profile of v0, /device:TPU:1, one launch (start us, length us, event | category | flops | bytes accessed | tf_op | source)
XLA Modules:
  0.0 167.6 jit_solution(1675939452613586958)
XLA Ops:
  2.3 3.3 %collective-permute-start.24 = (f32[5,16,128]{2,1,0:T(8,128)S(1)}, f32[5,16,128]{2,1,0:T(8,128)S(1)}, u32[]{:S(2)}, u32[]{:S(2)}) collective-permute-start(f32[5,16,128]{2,1,0:T(8,128)S(1)} %select_reduce_fusion.own_side), channel_id=1, source_target_pairs={{0,1},{1,0},{2,3},{3,2},{4,5},{5,4},{6,7},{7,6},{8,9},{9,8},{10,11... | collective-permute-start | bytes 122888 | tf_op jit(solution)/shard_map/ppermute | solution.py:24
  7.4 4.8 %shard_map.55 = (bf16[1,1024,128]{2,1,0:T(8,128)(2,1)}, bf16[2,1024,128]{2,1,0:T(8,128)(2,1)}, bf16[3,1024,128]{2,1,0:T(8,128)(2,1)}, bf16[4,1024,128]{2,1,0:T(8,128)(2,1)}, bf16[5,128,1024]{2,1,0:T(8,128)(2,1)}) custom-call(s32[13]{0:T(128)} %concatenate.195.at_ref, bf16[5,4096,128]{2,1,0:T(8,128)(2,1)} %bitcast.75, bf16[5,4096,128]{2,1,0:T(8,128)(2,1)} %bitcast.76, ...), custom_call_target="tpu_custom_call" | custom-call | bytes 7340032 | tf_op jit(solution)/shard_map/pallas_call | solution.py:54
  14.1 6.5 %all-to-all-start = ((f32[8,8,128]{2,1,0:T(8,128)}), f32[8,8,128]{2,1,0:T(8,128)S(1)}, u32[]{:S(2)}, u32[]{:S(2)}) async-start(f32[8,8,128]{2,1,0:T(8,128)} %broadcast_in_dim.172), calls=%async_computation | async-start | bytes 65536 | tf_op jit(solution)/shard_map/all_to_all | solution.py:19
  31.5 4.0 %conditional.8 = (bf16[1,16,128]{2,1,0:T(8,128)(2,1)S(1)}) conditional(s32[]{:T(128)} %clamp.31, bf16[1,16,128]{2,1,0:T(8,128)(2,1)S(1)} %fusion.18, bf16[1,16,128]{2,1,0:T(8,128)(2,1)S(1)} %fusion.18, bf16[1,16,128]{2,1,0:T(8,128)(2,1)S(1)} %fusion.18, bf16[1,16,128]{2,1,0:T(8,128)(2,1)S(1)} %fusion.18), branch_computations={%region_2.3_spmd, %region_3.4_spmd, %region_4.5_spmd, %region_5.6_... | conditional | bytes 24624 | solution.py:37
  31.5 3.0 %collective-permute-start.1 = (bf16[1,16,128]{2,1,0:T(8,128)(2,1)S(1)}, bf16[1,16,128]{2,1,0:T(8,128)(2,1)S(1)}, u32[]{:S(2)}, u32[]{:S(2)}) collective-permute-start(bf16[1,16,128]{2,1,0:T(8,128)(2,1)S(1)} %param.2), channel_id=1, source_target_pairs={{0,16},{1,17},{2,18},{3,19},{4,20},{5,21},{6,22},{7,23},{8,24},{9,... | collective-permute-start | bytes 12296 | tf_op jit(solution)/shard_map/cond/branch_2_fun/ppermute | solution.py:24
  37.3 14.2 %all_to_all.35 = f32[8,8,1024]{2,1,0:T(8,128)S(1)} all-to-all(f32[8,8,1024]{2,1,0:T(8,128)S(1)} %shard_map.56), channel_id=1, replica_groups=mesh['row'=8,'col'=32] {'row'}, dimensions={0} | all-to-all | bytes 524288 | tf_op jit(solution)/shard_map/all_to_all | solution.py:227
  52.7 3.2 %collective-permute-start.30 = (f32[8,128]{1,0:T(8,128)S(1)}, f32[8,128]{1,0:T(8,128)S(1)}, u32[]{:S(2)}, u32[]{:S(2)}) collective-permute-start(f32[8,128]{1,0:T(8,128)S(1)} %fusion.6), channel_id=1, source_target_pairs={{0,1},{1,0},{2,3},{3,2},{4,5},{5,4},{6,7},{7,6},{8,9},{9,8},{10,11... | collective-permute-start | bytes 12296 | tf_op jit(solution)/shard_map/ppermute | solution.py:24
  56.9 2.6 %conditional.10 = (bf16[2,16,128]{2,1,0:T(8,128)(2,1)S(1)}) conditional(s32[]{:T(128)} %clamp.29, bf16[2,16,128]{2,1,0:T(8,128)(2,1)S(1)} %pad_maximum_fusion.3, bf16[2,16,128]{2,1,0:T(8,128)(2,1)S(1)} %pad_maximum_fusion.3, bf16[2,16,128]{2,1,0:T(8,128)(2,1)S(1)} %pad_maximum_fusion.3, ...), branch_computations={%region_11.12_spmd, %region_12.13_spmd, %region_13.14_spmd, %regio... | conditional | bytes 49200 | solution.py:37
  59.5 4.0 %conditional.11 = (bf16[2,16,128]{2,1,0:T(8,128)(2,1)S(1)}) conditional(s32[]{:T(128)} %clamp.28, bf16[2,16,128]{2,1,0:T(8,128)(2,1)S(1)} %get-tuple-element.202, bf16[2,16,128]{2,1,0:T(8,128)(2,1)S(1)} %get-tuple-element.202, bf16[2,16,128]{2,1,0:T(8,128)(2,1)S(1)} %get-tuple-element.202, ...), branch_computations={%region_15.16_spmd, %region_16.17_spmd, %region_17.18_spmd, %regio... | conditional | bytes 49200 | solution.py:37
  59.5 2.7 %collective-permute-start.10 = (bf16[2,16,128]{2,1,0:T(8,128)(2,1)S(1)}, bf16[2,16,128]{2,1,0:T(8,128)(2,1)S(1)}, u32[]{:S(2)}, u32[]{:S(2)}) collective-permute-start(bf16[2,16,128]{2,1,0:T(8,128)(2,1)S(1)} %param.14), channel_id=1, source_target_pairs={{0,4},{1,5},{2,6},{3,7},{4,0},{5,1},{6,2},{7,3},{8,12},{9,13},{10,... | collective-permute-start | bytes 24584 | tf_op jit(solution)/shard_map/cond/branch_2_fun/ppermute | solution.py:24
  65.4 11.8 %all_to_all.36 = f32[8,8,1024]{2,1,0:T(8,128)S(1)} all-to-all(f32[8,8,1024]{2,1,0:T(8,128)S(1)} %shard_map.57), channel_id=1, replica_groups=mesh['row'=8,'col'=32] {'row'}, dimensions={0} | all-to-all | bytes 524288 | tf_op jit(solution)/shard_map/all_to_all | solution.py:227
  78.5 3.8 %collective-permute-start.31 = (f32[8,128]{1,0:T(8,128)S(1)}, f32[8,128]{1,0:T(8,128)S(1)}, u32[]{:S(2)}, u32[]{:S(2)}) collective-permute-start(f32[8,128]{1,0:T(8,128)S(1)} %fusion.4), channel_id=1, source_target_pairs={{0,1},{1,0},{2,3},{3,2},{4,5},{5,4},{6,7},{7,6},{8,9},{9,8},{10,11... | collective-permute-start | bytes 12296 | tf_op jit(solution)/shard_map/ppermute | solution.py:24
  83.2 3.9 %conditional.13 = (bf16[3,16,128]{2,1,0:T(8,128)(2,1)S(1)}) conditional(s32[]{:T(128)} %clamp.26, bf16[3,16,128]{2,1,0:T(8,128)(2,1)S(1)} %get-tuple-element.204, bf16[3,16,128]{2,1,0:T(8,128)(2,1)S(1)} %get-tuple-element.204, bf16[3,16,128]{2,1,0:T(8,128)(2,1)S(1)} %get-tuple-element.204, ...), branch_computations={%region_24.25_spmd, %region_25.26_spmd, %region_26.27_spmd, %regio... | conditional | bytes 73776 | solution.py:37
  89.2 12.6 %all_to_all.37 = f32[8,8,1024]{2,1,0:T(8,128)S(1)} all-to-all(f32[8,8,1024]{2,1,0:T(8,128)S(1)} %shard_map.58), channel_id=1, replica_groups=mesh['row'=8,'col'=32] {'row'}, dimensions={0} | all-to-all | bytes 524288 | tf_op jit(solution)/shard_map/all_to_all | solution.py:227
  103.0 2.6 %collective-permute-start.32 = (f32[8,128]{1,0:T(8,128)S(1)}, f32[8,128]{1,0:T(8,128)S(1)}, u32[]{:S(2)}, u32[]{:S(2)}) collective-permute-start(f32[8,128]{1,0:T(8,128)S(1)} %fusion.2), channel_id=1, source_target_pairs={{0,1},{1,0},{2,3},{3,2},{4,5},{5,4},{6,7},{7,6},{8,9},{9,8},{10,11... | collective-permute-start | bytes 12296 | tf_op jit(solution)/shard_map/ppermute | solution.py:24
  106.7 4.2 %conditional.14 = (bf16[4,16,128]{2,1,0:T(8,128)(2,1)S(1)}) conditional(s32[]{:T(128)} %clamp.25, bf16[4,16,128]{2,1,0:T(8,128)(2,1)S(1)} %pad_maximum_fusion.1, bf16[4,16,128]{2,1,0:T(8,128)(2,1)S(1)} %pad_maximum_fusion.1, bf16[4,16,128]{2,1,0:T(8,128)(2,1)S(1)} %pad_maximum_fusion.1, ...), branch_computations={%region_29.30_spmd, %region_30.31_spmd, %region_31.32_spmd, %regio... | conditional | bytes 98352 | solution.py:37
  106.7 3.0 %collective-permute-start.19 = (bf16[4,16,128]{2,1,0:T(8,128)(2,1)S(1)}, bf16[4,16,128]{2,1,0:T(8,128)(2,1)S(1)}, u32[]{:S(2)}, u32[]{:S(2)}) collective-permute-start(bf16[4,16,128]{2,1,0:T(8,128)(2,1)S(1)} %param.26), channel_id=1, source_target_pairs={{0,16},{1,17},{2,18},{3,19},{4,20},{5,21},{6,22},{7,23},{8,24},{9,... | collective-permute-start | bytes 49160 | tf_op jit(solution)/shard_map/cond/branch_2_fun/ppermute | solution.py:24
  110.8 2.6 %conditional.15 = (bf16[4,16,128]{2,1,0:T(8,128)(2,1)S(1)}) conditional(s32[]{:T(128)} %clamp.24, bf16[4,16,128]{2,1,0:T(8,128)(2,1)S(1)} %get-tuple-element.206, bf16[4,16,128]{2,1,0:T(8,128)(2,1)S(1)} %get-tuple-element.206, bf16[4,16,128]{2,1,0:T(8,128)(2,1)S(1)} %get-tuple-element.206, ...), branch_computations={%region_33.34_spmd, %region_34.35_spmd, %region_35.36_spmd, %regio... | conditional | bytes 98352 | solution.py:37
  110.9 2.6 %collective-permute-done.21 = bf16[4,16,128]{2,1,0:T(8,128)(2,1)S(1)} collective-permute-done((bf16[4,16,128]{2,1,0:T(8,128)(2,1)S(1)}, bf16[4,16,128]{2,1,0:T(8,128)(2,1)S(1)}, u32[]{:S(2)}, u32[]{:S(2)}) %collective-permute-start.21) | collective-permute-done | bytes 16416 | tf_op jit(solution)/shard_map/cond/branch_1_fun/ppermute | solution.py:24
  114.4 11.8 %all_to_all.38 = f32[8,8,1024]{2,1,0:T(8,128)S(1)} all-to-all(f32[8,8,1024]{2,1,0:T(8,128)S(1)} %shard_map.59), channel_id=1, replica_groups=mesh['row'=8,'col'=32] {'row'}, dimensions={0} | all-to-all | bytes 524288 | tf_op jit(solution)/shard_map/all_to_all | solution.py:227
  127.5 3.8 %collective-permute-start.33 = (f32[8,128]{1,0:T(8,128)S(1)}, f32[8,128]{1,0:T(8,128)S(1)}, u32[]{:S(2)}, u32[]{:S(2)}) collective-permute-start(f32[8,128]{1,0:T(8,128)S(1)} %fusion), channel_id=1, source_target_pairs={{0,1},{1,0},{2,3},{3,2},{4,5},{5,4},{6,7},{7,6},{8,9},{9,8},{10,11... | collective-permute-start | bytes 12296 | tf_op jit(solution)/shard_map/ppermute | solution.py:24
  132.3 15.3 %all_to_all.39.sent_ref = bf16[16,5,16,128]{3,2,1,0:T(8,128)(2,1)} all-to-all(bf16[16,5,16,128]{3,2,1,0:T(8,128)(2,1)S(1)} %broadcast_in_dim.198), channel_id=1, replica_groups={{0,2,4,6,8,10,12,14,16,18,20,22,24,26,28,30},{1,3,5,7,9,11,13,15,17,19,..., dimensions={0} | all-to-all | bytes 655360 | tf_op jit(solution)/shard_map/all_to_all | solution.py:19
  147.5 5.8 %shard_map.60 = f32[8,4,16,128]{3,2,1,0:T(8,128)} custom-call(s32[13]{0:T(128)} %concatenate.195.at_ref, bf16[16,5,16,128]{3,2,1,0:T(8,128)(2,1)} %all_to_all.39.sent_ref, bf16[5,4096,128]{2,1,0:T(8,128)(2,1)} %bitcast.79), custom_call_target="tpu_custom_call" | custom-call | flops 83886080 | bytes 5242880 | tf_op jit(solution)/shard_map/pallas_call | solution.py:144
  153.3 13.5 %all_to_all.40 = f32[8,4,16,128]{3,2,1,0:T(8,128)S(1)} all-to-all(f32[8,4,16,128]{3,2,1,0:T(8,128)} %shard_map.60), channel_id=1, replica_groups=mesh['row'=8,'col'=32] {'row'}, dimensions={0} | all-to-all | bytes 524288 | tf_op jit(solution)/shard_map/all_to_all | solution.py:249
  (106 shorter events, 37.4 us)
Async XLA Ops:
  2.3 11.2 %collective-permute-start.24 = (f32[5,16,128]{2,1,0:T(8,128)S(1)}, f32[5,16,128]{2,1,0:T(8,128)S(1)}, u32[]{:S(2)}, u32[]{:S(2)}) collective-permute-start(f32[5,16,128]{2,1,0:T(8,128)S(1)} %select_reduce_fusion.own_side), channel_id=1, source_target_pairs={{0,1},{1,0},{2,3},{3,2},{4,5},{5,4},{6,7},{7,6},{8,9},{9,8},{10,11... | collective-permute-start | bytes 122888 | tf_op jit(solution)/shard_map/ppermute | solution.py:24
  7.4 28.1 %copy-start.8 = (s32[13]{0:T(128)S(1)}, s32[13]{0:T(128)}, u32[]{:S(2)}) copy-start(s32[13]{0:T(128)} %concatenate.195.at_ref) | copy-start | bytes 160
  12.2 15.2 %collective-permute-start.25 = (bf16[1,1024,128]{2,1,0:T(8,128)(2,1)}, bf16[1,1024,128]{2,1,0:T(8,128)(2,1)S(1)}, u32[]{:S(2)}, u32[]{:S(2)}) collective-permute-start(bf16[1,1024,128]{2,1,0:T(8,128)(2,1)} %get-tuple-element.148.own_ref), channel_id=1, source_target_pairs={{0,1},{1,0},{2,3},{3,2},{4,5},{5,4},{6,7},{7,6},{8,9},{9,8},{10,11... | collective-permute-start | bytes 786440 | tf_op jit(solution)/shard_map/ppermute | solution.py:24
  12.3 15.2 %collective-permute-start.26 = (bf16[2,1024,128]{2,1,0:T(8,128)(2,1)}, bf16[2,1024,128]{2,1,0:T(8,128)(2,1)S(1)}, u32[]{:S(2)}, u32[]{:S(2)}) collective-permute-start(bf16[2,1024,128]{2,1,0:T(8,128)(2,1)} %get-tuple-element.157.own_ref), channel_id=1, source_target_pairs={{0,1},{1,0},{2,3},{3,2},{4,5},{5,4},{6,7},{7,6},{8,9},{9,8},{10,11... | collective-permute-start | bytes 1572872 | tf_op jit(solution)/shard_map/ppermute | solution.py:24
  12.7 14.7 %collective-permute-start.27 = (bf16[3,1024,128]{2,1,0:T(8,128)(2,1)}, bf16[3,1024,128]{2,1,0:T(8,128)(2,1)S(1)}, u32[]{:S(2)}, u32[]{:S(2)}) collective-permute-start(bf16[3,1024,128]{2,1,0:T(8,128)(2,1)} %get-tuple-element.164.own_ref), channel_id=1, source_target_pairs={{0,1},{1,0},{2,3},{3,2},{4,5},{5,4},{6,7},{7,6},{8,9},{9,8},{10,11... | collective-permute-start | bytes 2359304 | tf_op jit(solution)/shard_map/ppermute | solution.py:24
  12.8 14.7 %collective-permute-start.28 = (bf16[4,1024,128]{2,1,0:T(8,128)(2,1)}, bf16[4,1024,128]{2,1,0:T(8,128)(2,1)S(1)}, u32[]{:S(2)}, u32[]{:S(2)}) collective-permute-start(bf16[4,1024,128]{2,1,0:T(8,128)(2,1)} %get-tuple-element.171.own_ref), channel_id=1, source_target_pairs={{0,1},{1,0},{2,3},{3,2},{4,5},{5,4},{6,7},{7,6},{8,9},{9,8},{10,11... | collective-permute-start | bytes 3145736 | tf_op jit(solution)/shard_map/ppermute | solution.py:24
  14.1 13.4 %all-to-all-start = ((f32[8,8,128]{2,1,0:T(8,128)}), f32[8,8,128]{2,1,0:T(8,128)S(1)}, u32[]{:S(2)}, u32[]{:S(2)}) async-start(f32[8,8,128]{2,1,0:T(8,128)} %broadcast_in_dim.172), calls=%async_computation | async-start | bytes 65536 | tf_op jit(solution)/shard_map/all_to_all | solution.py:19
  27.5 29.4 %copy-start.5 = (bf16[2,1024,128]{2,1,0:T(8,128)(2,1)}, bf16[2,1024,128]{2,1,0:T(8,128)(2,1)S(1)}, u32[]{:S(2)}) copy-start(bf16[2,1024,128]{2,1,0:T(8,128)(2,1)S(1)} %collective-permute-done.26.other_ref) | copy-start | bytes 1572868
  27.5 29.4 %copy-start.2 = (bf16[3,1024,128]{2,1,0:T(8,128)(2,1)}, bf16[3,1024,128]{2,1,0:T(8,128)(2,1)S(1)}, u32[]{:S(2)}) copy-start(bf16[3,1024,128]{2,1,0:T(8,128)(2,1)S(1)} %collective-permute-done.27.other_ref) | copy-start | bytes 2359300
  27.5 36.0 %copy-start.4 = (bf16[2,1024,128]{2,1,0:T(8,128)(2,1)S(1)}, bf16[2,1024,128]{2,1,0:T(8,128)(2,1)}, u32[]{:S(2)}) copy-start(bf16[2,1024,128]{2,1,0:T(8,128)(2,1)} %get-tuple-element.157.own_ref) | copy-start | bytes 1572868
  29.0 2.3 %collective-permute-start.29 = (f32[8,128]{1,0:T(8,128)S(1)}, f32[8,128]{1,0:T(8,128)S(1)}, u32[]{:S(2)}, u32[]{:S(2)}) collective-permute-start(f32[8,128]{1,0:T(8,128)S(1)} %fusion.8), channel_id=1, source_target_pairs={{0,1},{1,0},{2,3},{3,2},{4,5},{5,4},{6,7},{7,6},{8,9},{9,8},{10,11... | collective-permute-start | bytes 12296 | tf_op jit(solution)/shard_map/ppermute | solution.py:24
  31.5 4.0 %collective-permute-start.1 = (bf16[1,16,128]{2,1,0:T(8,128)(2,1)S(1)}, bf16[1,16,128]{2,1,0:T(8,128)(2,1)S(1)}, u32[]{:S(2)}, u32[]{:S(2)}) collective-permute-start(bf16[1,16,128]{2,1,0:T(8,128)(2,1)S(1)} %param.2), channel_id=1, source_target_pairs={{0,16},{1,17},{2,18},{3,19},{4,20},{5,21},{6,22},{7,23},{8,24},{9,... | collective-permute-start | bytes 12296 | tf_op jit(solution)/shard_map/cond/branch_2_fun/ppermute | solution.py:24
  52.7 4.0 %collective-permute-start.30 = (f32[8,128]{1,0:T(8,128)S(1)}, f32[8,128]{1,0:T(8,128)S(1)}, u32[]{:S(2)}, u32[]{:S(2)}) collective-permute-start(f32[8,128]{1,0:T(8,128)S(1)} %fusion.6), channel_id=1, source_target_pairs={{0,1},{1,0},{2,3},{3,2},{4,5},{5,4},{6,7},{7,6},{8,9},{9,8},{10,11... | collective-permute-start | bytes 12296 | tf_op jit(solution)/shard_map/ppermute | solution.py:24
  56.9 2.6 %collective-permute-start.6 = (bf16[2,16,128]{2,1,0:T(8,128)(2,1)S(1)}, bf16[2,16,128]{2,1,0:T(8,128)(2,1)S(1)}, u32[]{:S(2)}, u32[]{:S(2)}) collective-permute-start(bf16[2,16,128]{2,1,0:T(8,128)(2,1)S(1)} %param.9), channel_id=1, source_target_pairs={{0,8},{1,9},{2,10},{3,11},{4,12},{5,13},{6,14},{7,15},{8,0},{9,1},... | collective-permute-start | bytes 24584 | tf_op jit(solution)/shard_map/cond/branch_1_fun/ppermute | solution.py:24
  59.5 4.0 %collective-permute-start.10 = (bf16[2,16,128]{2,1,0:T(8,128)(2,1)S(1)}, bf16[2,16,128]{2,1,0:T(8,128)(2,1)S(1)}, u32[]{:S(2)}, u32[]{:S(2)}) collective-permute-start(bf16[2,16,128]{2,1,0:T(8,128)(2,1)S(1)} %param.14), channel_id=1, source_target_pairs={{0,4},{1,5},{2,6},{3,7},{4,0},{5,1},{6,2},{7,3},{8,12},{9,13},{10,... | collective-permute-start | bytes 24584 | tf_op jit(solution)/shard_map/cond/branch_2_fun/ppermute | solution.py:24
  64.6 22.5 %copy-start.1 = (bf16[3,1024,128]{2,1,0:T(8,128)(2,1)S(1)}, bf16[3,1024,128]{2,1,0:T(8,128)(2,1)}, u32[]{:S(2)}) copy-start(bf16[3,1024,128]{2,1,0:T(8,128)(2,1)} %get-tuple-element.164.own_ref) | copy-start | bytes 2359300
  78.5 4.6 %collective-permute-start.31 = (f32[8,128]{1,0:T(8,128)S(1)}, f32[8,128]{1,0:T(8,128)S(1)}, u32[]{:S(2)}, u32[]{:S(2)}) collective-permute-start(f32[8,128]{1,0:T(8,128)S(1)} %fusion.4), channel_id=1, source_target_pairs={{0,1},{1,0},{2,3},{3,2},{4,5},{5,4},{6,7},{7,6},{8,9},{9,8},{10,11... | collective-permute-start | bytes 12296 | tf_op jit(solution)/shard_map/ppermute | solution.py:24
  83.3 3.8 %collective-permute-start.17 = (bf16[3,16,128]{2,1,0:T(8,128)(2,1)S(1)}, bf16[3,16,128]{2,1,0:T(8,128)(2,1)S(1)}, u32[]{:S(2)}, u32[]{:S(2)}) collective-permute-start(bf16[3,16,128]{2,1,0:T(8,128)(2,1)S(1)} %param.23), channel_id=1, source_target_pairs={{0,6},{1,7},{2,4},{3,5},{4,2},{5,3},{6,0},{7,1},{8,14},{9,15},{10,... | collective-permute-start | bytes 36872 | tf_op jit(solution)/shard_map/cond/branch_3_fun/ppermute | solution.py:24
  88.2 25.2 %copy-start = (bf16[4,1024,128]{2,1,0:T(8,128)(2,1)S(1)}, bf16[4,1024,128]{2,1,0:T(8,128)(2,1)}, u32[]{:S(2)}) copy-start(bf16[4,1024,128]{2,1,0:T(8,128)(2,1)} %get-tuple-element.171.own_ref) | copy-start | bytes 3145732
  103.0 3.5 %collective-permute-start.32 = (f32[8,128]{1,0:T(8,128)S(1)}, f32[8,128]{1,0:T(8,128)S(1)}, u32[]{:S(2)}, u32[]{:S(2)}) collective-permute-start(f32[8,128]{1,0:T(8,128)S(1)} %fusion.2), channel_id=1, source_target_pairs={{0,1},{1,0},{2,3},{3,2},{4,5},{5,4},{6,7},{7,6},{8,9},{9,8},{10,11... | collective-permute-start | bytes 12296 | tf_op jit(solution)/shard_map/ppermute | solution.py:24
  106.7 4.2 %collective-permute-start.19 = (bf16[4,16,128]{2,1,0:T(8,128)(2,1)S(1)}, bf16[4,16,128]{2,1,0:T(8,128)(2,1)S(1)}, u32[]{:S(2)}, u32[]{:S(2)}) collective-permute-start(bf16[4,16,128]{2,1,0:T(8,128)(2,1)S(1)} %param.26), channel_id=1, source_target_pairs={{0,16},{1,17},{2,18},{3,19},{4,20},{5,21},{6,22},{7,23},{8,24},{9,... | collective-permute-start | bytes 49160 | tf_op jit(solution)/shard_map/cond/branch_2_fun/ppermute | solution.py:24
  110.8 2.6 %collective-permute-start.21 = (bf16[4,16,128]{2,1,0:T(8,128)(2,1)S(1)}, bf16[4,16,128]{2,1,0:T(8,128)(2,1)S(1)}, u32[]{:S(2)}, u32[]{:S(2)}) collective-permute-start(bf16[4,16,128]{2,1,0:T(8,128)(2,1)S(1)} %param.29), channel_id=1, source_target_pairs={{0,2},{1,3},{2,0},{3,1},{4,6},{5,7},{6,4},{7,5},{8,10},{9,11},{10,... | collective-permute-start | bytes 49160 | tf_op jit(solution)/shard_map/cond/branch_1_fun/ppermute | solution.py:24
  127.5 4.6 %collective-permute-start.33 = (f32[8,128]{1,0:T(8,128)S(1)}, f32[8,128]{1,0:T(8,128)S(1)}, u32[]{:S(2)}, u32[]{:S(2)}) collective-permute-start(f32[8,128]{1,0:T(8,128)S(1)} %fusion), channel_id=1, source_target_pairs={{0,1},{1,0},{2,3},{3,2},{4,5},{5,4},{6,7},{7,6},{8,9},{9,8},{10,11... | collective-permute-start | bytes 12296 | tf_op jit(solution)/shard_map/ppermute | solution.py:24
  147.5 19.3 %copy-start.9 = (f32[16,4,128]{2,1,0:T(4,128)S(1)}, f32[16,4,128]{2,1,0:T(4,128)}, u32[]{:S(2)}) copy-start(f32[16,4,128]{2,1,0:T(4,128)} %param.39) | copy-start | bytes 98308
  (4 other events, 9.0 us)
where the time goes:
time: 169 us; the launch traced here: 168 us
  blocking collectives  79.2 us (47%)
  starting transfers between devices  38.2 us (23%)
  Pallas kernels  14.1 us (8%)
  waiting for transfers between devices  13.8 us (8%)
  local copies, waits for them, and re-layouts  7.1 us (4%)
  matrix products  6.51 us (4%)
  between operations  5.92 us (4%)
  other arithmetic  2.67 us (2%)
    all_to_all x4, blocking collectives, per_device(): remaining = lax.all_to_all(copies, 'row', 0, 0, tiled=True).sum(axis=0)  50.4 us
    ppermute x16, starting transfers between devices, from_mask(): return lax.ppermute(array, 'col', [(i, i ^ mask) for i in range(size)])  31.7 us
    all_to_all x1, blocking collectives, to_all(): lax.all_to_all(copies, axis, 0, 0, axis_index_groups=groups, tiled=True)  15.3 us
    all_to_all x1, blocking collectives, per_device(): total = lax.all_to_all(pieces, 'row', 0, 0, tiled=True).sum(axis=0)  13.5 us
    ppermute x16, waiting for transfers between devices, from_mask(): return lax.ppermute(array, 'col', [(i, i ^ mask) for i in range(size)])  12.7 us
    dot_general x5, matrix products, per_device(): lax.dot_general(remaining, inverses[section].astype(F32), NT, precision=l...  6.51 us
    all_to_all x1, starting transfers between devices, to_all(): lax.all_to_all(copies, axis, 0, 0, axis_index_groups=groups, tiled=True)  6.48 us
    pallas_call x1, Pallas kernels, trailing(): pl.pallas_call(trailing_kernel, out_shape=jax.ShapeDtypeStruct((peers, ti...  5.76 us
  transfers between devices with their start and end apart: 17, of which 12 were waited for; matrix products, arithmetic and copies ran while one was open for 2% of the time, Pallas kernels for 3%

commit v1 on v0

--- a/solution.py
+++ b/solution.py
@@ -38,37 +38,46 @@
     return array
 
 
-def window_kernel(at_ref, *refs):
-    count = len(refs) // 2
-    for rows_ref, out_ref in zip(refs[:count], refs[count:], strict=True):
-        out_ref[...] = rows_ref[...]
+def window_kernel(at_ref, factor_ref, diag_ref, *refs):
+    *row_refs, inverse_ref, sems = refs
+    tile_width = row_refs[0].shape[1]
+    copies = []
+    for t, out_ref in enumerate(row_refs, 1):
+        start = pl.multiple_of(at_ref[PLACE + t] * tile_width, tile_width)
+        rows = factor_ref.at[pl.ds(0, t), pl.ds(start, tile_width), :]
+        copies.append(pltpu.make_async_copy(rows, out_ref, sems.at[t]))
+    copies.append(pltpu.make_async_copy(diag_ref.at[0], inverse_ref, sems.at[0]))
+    for copy in copies:
+        copy.start()
+    for copy in copies:
+        copy.wait()
 
 
 def window_rows(at, factor, diag_inverse):
     section_count, width, tile_width = diag_inverse.shape
-
-    def spec(section, index_map):
-        return pl.BlockSpec((section, tile_width, width), index_map)
-
-    later = range(1, section_count)
+    shapes = [(t, tile_width, width) for t in range(1, section_count)] + [(width, tile_width)]
+    in_place = pl.BlockSpec(memory_space=pltpu.HBM)
     return pl.pallas_call(
         window_kernel,
-        out_shape=[jax.ShapeDtypeStruct((t, tile_width, width), factor.dtype) for t in later]
-        + [jax.ShapeDtypeStruct(diag_inverse.shape, diag_inverse.dtype)],
+        out_shape=[jax.ShapeDtypeStruct(shape, factor.dtype) for shape in shapes],
         grid_spec=pltpu.PrefetchScalarGridSpec(
             num_scalar_prefetch=1,
             grid=(1,),
-            in_specs=[spec(t, lambda i, at, t=t: (0, at[PLACE + t], 0)) for t in later]
-            + [pl.BlockSpec(diag_inverse.shape, lambda i, at: (0, 0, 0))],
-            out_specs=[spec(t, lambda i, at: (0, 0, 0)) for t in later]
-            + [pl.BlockSpec(diag_inverse.shape, lambda i, at: (0, 0, 0))],
-        ),
-        compiler_params=pltpu.CompilerParams(vmem_limit_bytes=60 << 20),
-        cost_estimate=pl.CostEstimate(flops=0, bytes_accessed=7 << 20, transcendentals=0),
-    )(at, *[factor for _ in later], diag_inverse)
-
-
-def partial_kernel(section, at_ref, sent_ref, own_ref, other_ref, own_side, other_side, out_ref):
+            in_specs=[in_place, in_place],
+            out_specs=[
+                pl.BlockSpec(shape, lambda i, at, rank=len(shape): (0,) * rank) for shape in shapes
+            ],
+            scratch_shapes=[pltpu.SemaphoreType.DMA((section_count,))],
+        ),
+        compiler_params=pltpu.CompilerParams(vmem_limit_bytes=8 << 20),
+        cost_estimate=pl.CostEstimate(flops=0, bytes_accessed=5 << 20, transcendentals=0),
+    )(at, factor, diag_inverse)
+
+
+def partial_kernel(
+    section, at_ref, sent_ref, own_ref, other_ref, own_side, other_side, diag_ref, out_ref, inverse_ref
+):
+    inverse_ref[...] = diag_ref[0]
     me, core = at_ref[0], at_ref[1]
     peers, half, _ = out_ref.shape
     width = own_side.shape[2]
@@ -97,7 +106,7 @@
         write(other_ref, other_side)
 
 
-def partial_half(section, at, sent, own_rows, other_rows, own_sides, other_sides, peers):
+def partial_half(section, at, sent, own_rows, other_rows, own_sides, other_sides, diag_inverse, peers):
     _, rhs_count, width = sent.shape
     tile_width = own_rows.shape[1]
     half = rhs_count // 2
@@ -105,7 +114,10 @@
     side = pl.BlockSpec((1, rhs_count, width), lambda i, at: (section, 0, 0))
     return pl.pallas_call(
         functools.partial(partial_kernel, section),
-        out_shape=jax.ShapeDtypeStruct((peers, half, tile_width), F32),
+        out_shape=[
+            jax.ShapeDtypeStruct((peers, half, tile_width), F32),
+            jax.ShapeDtypeStruct((width, tile_width), diag_inverse.dtype),
+        ],
         grid_spec=pltpu.PrefetchScalarGridSpec(
             num_scalar_prefetch=1,
             grid=(1,),
@@ -115,8 +127,12 @@
                 rows,
                 side,
                 side,
-            ],
-            out_specs=pl.BlockSpec((peers, half, tile_width), lambda i, at: (0, 0, 0)),
+                pl.BlockSpec((1, width, tile_width), lambda i, at: (section, 0, 0)),
+            ],
+            out_specs=[
+                pl.BlockSpec((peers, half, tile_width), lambda i, at: (0, 0, 0)),
+                pl.BlockSpec((width, tile_width), lambda i, at: (0, 0)),
+            ],
         ),
         compiler_params=pltpu.CompilerParams(vmem_limit_bytes=8 << 20),
         cost_estimate=pl.CostEstimate(
@@ -124,18 +140,31 @@
             bytes_accessed=4 * section * width * tile_width,
             transcendentals=0,
         ),
-    )(at, sent, own_rows, other_rows, own_sides, other_sides)
-
-
-def trailing_kernel(at_ref, sent_ref, rows_ref, out_ref):
-    total = lax.dot_general(sent_ref[0, 0], rows_ref[0], NT, preferred_element_type=F32)
-    for before in range(1, rows_ref.shape[0]):
-        total = total + lax.dot_general(
-            sent_ref[0, before], rows_ref[before], NT, preferred_element_type=F32
+    )(at, sent, own_rows, other_rows, own_sides, other_sides, diag_inverse)
+
+
+def trailing_kernel(at_ref, sent_ref, factor_ref, out_ref, rows, sems):
+    peers, tiles, _, width = out_ref.shape
+    tile_width = peers * width
+    copies = []
+    for tile in range(tiles):
+        span = pl.ds(tile * tile_width, tile_width)
+        copies.append(
+            pltpu.make_async_copy(factor_ref.at[:, span, :], rows.at[:, span, :], sems.at[tile])
         )
-    width = out_ref.shape[3]
-    for peer in range(out_ref.shape[0]):
-        out_ref[peer, 0] = total[:, peer * width : (peer + 1) * width]
+    for copy in copies:
+        copy.start()
+    for tile in range(tiles):
+        copies[tile].wait()
+        span = pl.ds(tile * tile_width, tile_width)
+        total = None
+        for before in range(rows.shape[0]):
+            term = lax.dot_general(
+                sent_ref[0, before], rows[before, span, :], NT, preferred_element_type=F32
+            )
+            total = term if total is None else total + term
+        for peer in range(peers):
+            out_ref[peer, tile] = total[:, peer * width : (peer + 1) * width]
 
 
 def trailing(at, sent, factor, tile_width, peers):
@@ -146,14 +175,18 @@
         out_shape=jax.ShapeDtypeStruct((peers, tiles, rhs_count, width), F32),
         grid_spec=pltpu.PrefetchScalarGridSpec(
             num_scalar_prefetch=1,
-            grid=(tiles,),
+            grid=(1,),
             in_specs=[
                 pl.BlockSpec((1, count, rhs_count, width), lambda i, at: (at[CHIP], 0, 0, 0)),
-                pl.BlockSpec((count, tile_width, width), lambda i, at: (0, i, 0)),
-            ],
-            out_specs=pl.BlockSpec((peers, 1, rhs_count, width), lambda i, at: (0, i, 0, 0)),
-        ),
-        compiler_params=pltpu.CompilerParams(vmem_limit_bytes=60 << 20),
+                pl.BlockSpec(memory_space=pltpu.HBM),
+            ],
+            out_specs=pl.BlockSpec((peers, tiles, rhs_count, width), lambda i, at: (0, 0, 0, 0)),
+            scratch_shapes=[
+                pltpu.VMEM(factor.shape, factor.dtype),
+                pltpu.SemaphoreType.DMA((tiles,)),
+            ],
+        ),
+        compiler_params=pltpu.CompilerParams(vmem_limit_bytes=12 << 20),
         cost_estimate=pl.CostEstimate(
             flops=2 * count * rhs_count * width * tile_width * tiles,
             bytes_accessed=2 * count * width * tile_width * tiles,
@@ -190,21 +223,18 @@
     chip = lax.shift_right_logical(owner[-1], jnp.int32(1))
     head = jnp.stack([me, core, chip])
     at = jnp.concatenate([head, place, mine.astype(jnp.int32)]).astype(jnp.int32)
-    *own_rows, inverses = window_rows(at, factor, diag_inverse)
+    *own_rows, inverse = window_rows(at, factor, diag_inverse)
     other_rows = [from_mask(rows, 1) for rows in own_rows]
     masks = owner[1:] ^ owner[:-1]
     parts = [
-        [
-            lax.shift_right_logical(masks[section], jnp.int32(low)) & ((1 << bits) - 1)
-            for low, bits in levels(cols)
-        ]
-        for section in range(section_count - 1)
+        lax.shift_right_logical(masks, jnp.int32(low)) & ((1 << bits) - 1)
+        for low, bits in levels(cols)
     ]
     live = order[:, None] < live_segments[None, :]
     taken = (here & mine[:, None])[:, None, :] & live[:, :, None]
     done = taken.any(axis=0)[:, :, None]
-    first = (arrived, parts, at, live, taken, done, sides, other_sides, own_rows, other_rows, inverses)
-    arrived, parts, at, live, taken, done, sides, other_sides, own_rows, other_rows, inverses = (
+    first = (arrived, at, live, taken, done, sides, other_sides, own_rows, other_rows, inverse)
+    arrived, at, live, taken, done, sides, other_sides, own_rows, other_rows, inverse = (
         lax.optimization_barrier(first)
     )
 
@@ -213,7 +243,7 @@
     result = jnp.zeros_like(right_side)
     for section in range(section_count):
         if section:
-            copies = partial_half(
+            copies, inverse = partial_half(
                 section,
                 at,
                 history,
@@ -221,13 +251,16 @@
                 other_rows[section - 1],
                 sides,
                 other_sides,
+                diag_inverse,
                 peers,
             )
-            copies, history, result = lax.optimization_barrier((copies, history, result))
+            copies, inverse, history, result = lax.optimization_barrier(
+                (copies, inverse, history, result)
+            )
             remaining = lax.all_to_all(copies, "row", 0, 0, tiled=True).sum(axis=0)
         solved = lax.dot_general(
             remaining,
-            inverses[section].astype(F32),
+            inverse.astype(F32),
             NT,
             precision=lax.Precision.HIGHEST,
             preferred_element_type=F32,
@@ -241,7 +274,7 @@
         history = sent if history is None else jnp.concatenate([history, sent])
         if section < section_count - 1:
             history, result = lax.optimization_barrier((history, result))
-            history = moved_by_mask(history, parts[section])
+            history = moved_by_mask(history, [part[section] for part in parts])
     history, result = lax.optimization_barrier((history, result))
     planes = [list(range(first, cols, 2)) for first in range(2)]
     everywhere = to_all(history, "col", cols // 2, planes)

time: 169 us -> 181 us (1.071)
  other arithmetic: 2.67 us -> 11.6 us
  local copies, waits for them, and re-layouts: 7.1 us -> 14.4 us
  Pallas kernels: 14.1 us -> 12.1 us
    unnamed x23, local copies, waits for them, and re-layouts: 3.91 us -> 10.6 us
    select_n x5, other arithmetic: 0.39 us -> 4.52 us  [per_device(): result = jnp.where(taken[section][..., None], solved[:, None, :], result)]
    all_to_all x1, waiting for transfers between devices: 1.11 us -> 4.93 us  [to_all(): lax.all_to_all(copies, axis, 0, 0, axis_index_groups=groups, tiled=True)]
    ppermute x16, waiting for transfers between devices: 12.7 us -> 9.64 us  [from_mask(): return lax.ppermute(array, 'col', [(i, i ^ mask) for i in range(size)])]
    pallas_call x1, Pallas kernels: 5.76 us -> 2.75 us  [trailing(): pl.pallas_call(trailing_kernel, out_shape=jax.ShapeDtypeStruct((peers, ti...]
    reduce_sum x4, other arithmetic: 0.07 us -> 2.94 us  [per_device(): remaining = lax.all_to_all(copies, 'row', 0, 0, tiled=True).sum(axis=0)]
    convert_element_type x5, other arithmetic: 0.37 us -> 2.32 us  [per_device(): sent = jnp.where(live[section][:, None], solved, 0.0).astype(BF16)[None]]
  transfers between devices with their start and end apart: 17 -> 17, of which waited for: 12 -> 9; matrix products, arithmetic and copies ran while one was open for 2% -> 1% of each run, Pallas kernels for 3% -> 1%
where the time goes in v1:
time: 181 us; the launch traced here: 180 us
  blocking collectives  79 us (44%)
  starting transfers between devices  36.7 us (20%)
  waiting for transfers between devices  14.6 us (8%)
  local copies, waits for them, and re-layouts  14.4 us (8%)
  Pallas kernels  12.1 us (7%)
  other arithmetic  11.6 us (6%)
  matrix products  6.25 us (3%)
  between operations  5.62 us (3%)
    all_to_all x4, blocking collectives, per_device(): remaining = lax.all_to_all(copies, 'row', 0, 0, tiled=True).sum(axis=0)  51.2 us
    ppermute x16, starting transfers between devices, from_mask(): return lax.ppermute(array, 'col', [(i, i ^ mask) for i in range(size)])  30.2 us
    all_to_all x1, blocking collectives, to_all(): lax.all_to_all(copies, axis, 0, 0, axis_index_groups=groups, tiled=True)  15.1 us
    all_to_all x1, blocking collectives, per_device(): total = lax.all_to_all(pieces, 'row', 0, 0, tiled=True).sum(axis=0)  12.6 us
    unnamed x23, local copies, waits for them, and re-layouts  10.6 us
    ppermute x16, waiting for transfers between devices, from_mask(): return lax.ppermute(array, 'col', [(i, i ^ mask) for i in range(size)])  9.64 us
    pallas_call x4, Pallas kernels, partial_half(): pl.pallas_call(functools.partial(partial_kernel, section), out_shape=[jax...  7.33 us
    all_to_all x1, starting transfers between devices, to_all(): lax.all_to_all(copies, axis, 0, 0, axis_index_groups=groups, tiled=True)  6.48 us
  transfers between devices with their start and end apart: 17, of which 9 were waited for; matrix products, arithmetic and copies ran while one was open for 1% of the time, Pallas kernels for 1%

profile of v1, /device:TPU:1, one launch (start us, length us, event | category | flops | bytes accessed | tf_op | source)
XLA Modules:
  0.0 180.2 jit_solution(10087745845206984415)
XLA Ops:
  2.3 3.3 %collective-permute-start.24 = (f32[5,16,128]{2,1,0:T(8,128)S(1)}, f32[5,16,128]{2,1,0:T(8,128)S(1)}, u32[]{:S(2)}, u32[]{:S(2)}) collective-permute-start(f32[5,16,128]{2,1,0:T(8,128)S(1)} %select_reduce_fusion.own_side), channel_id=1, source_target_pairs={{0,1},{1,0},{2,3},{3,2},{4,5},{5,4},{6,7},{7,6},{8,9},{9,8},{10,11... | collective-permute-start | bytes 122888 | tf_op jit(solution)/shard_map/ppermute | solution.py:24
  15.2 6.5 %all-to-all-start = ((f32[8,8,128]{2,1,0:T(8,128)}), f32[8,8,128]{2,1,0:T(8,128)S(1)}, u32[]{:S(2)}, u32[]{:S(2)}) async-start(f32[8,8,128]{2,1,0:T(8,128)} %broadcast_in_dim.172), calls=%async_computation | async-start | bytes 65536 | tf_op jit(solution)/shard_map/all_to_all | solution.py:19
  23.6 4.9 %all-to-all-done = f32[8,8,128]{2,1,0:T(8,128)S(1)} async-done(((f32[8,8,128]{2,1,0:T(8,128)}), f32[8,8,128]{2,1,0:T(8,128)S(1)}, u32[]{:S(2)}, u32[]{:S(2)}) %all-to-all-start) | async-done | bytes 32800 | tf_op jit(solution)/shard_map/all_to_all | solution.py:19
  33.5 4.0 %conditional.8 = (bf16[1,16,128]{2,1,0:T(8,128)(2,1)S(1)}) conditional(s32[]{:T(128)} %bitcast.14, bf16[1,16,128]{2,1,0:T(8,128)(2,1)S(1)} %fusion.4, bf16[1,16,128]{2,1,0:T(8,128)(2,1)S(1)} %fusion.4, bf16[1,16,128]{2,1,0:T(8,128)(2,1)S(1)} %fusion.4, bf16[1,16,128]{2,1,0:T(8,128)(2,1)S(1)} %fusion.4), branch_computations={%region_2.3_spmd, %region_3.4_spmd, %region_4.5_spmd, %region_5.6_... | conditional | bytes 24624 | solution.py:37
  33.5 3.0 %collective-permute-start.1 = (bf16[1,16,128]{2,1,0:T(8,128)(2,1)S(1)}, bf16[1,16,128]{2,1,0:T(8,128)(2,1)S(1)}, u32[]{:S(2)}, u32[]{:S(2)}) collective-permute-start(bf16[1,16,128]{2,1,0:T(8,128)(2,1)S(1)} %param.2), channel_id=1, source_target_pairs={{0,16},{1,17},{2,18},{3,19},{4,20},{5,21},{6,22},{7,23},{8,24},{9,... | collective-permute-start | bytes 12296 | tf_op jit(solution)/shard_map/cond/branch_2_fun/ppermute | solution.py:24
  40.1 13.3 %all_to_all.35 = f32[8,8,1024]{2,1,0:T(8,128)} all-to-all(f32[8,8,1024]{2,1,0:T(8,128)S(1)} %get-tuple-element.152), channel_id=1, replica_groups=mesh['row'=8,'col'=32] {'row'}, dimensions={0} | all-to-all | bytes 524288 | tf_op jit(solution)/shard_map/all_to_all | solution.py:260
  55.5 2.6 %collective-permute-start.30 = (f32[8,128]{1,0:T(8,128)S(1)}, f32[8,128]{1,0:T(8,128)S(1)}, u32[]{:S(2)}, u32[]{:S(2)}) collective-permute-start(f32[8,128]{1,0:T(8,128)S(1)} %fusion.18), channel_id=1, source_target_pairs={{0,1},{1,0},{2,3},{3,2},{4,5},{5,4},{6,7},{7,6},{8,9},{9,8},{10,11... | collective-permute-start | bytes 12296 | tf_op jit(solution)/shard_map/ppermute | solution.py:24
  61.0 2.5 %conditional.10 = (bf16[2,16,128]{2,1,0:T(8,128)(2,1)S(1)}) conditional(s32[]{:T(128)} %bitcast.12, bf16[2,16,128]{2,1,0:T(8,128)(2,1)S(1)} %pad_maximum_fusion.3, bf16[2,16,128]{2,1,0:T(8,128)(2,1)S(1)} %pad_maximum_fusion.3, bf16[2,16,128]{2,1,0:T(8,128)(2,1)S(1)} %pad_maximum_fusion.3, ...), branch_computations={%region_11.12_spmd, %region_12.13_spmd, %region_13.14_spmd, %regio... | conditional | bytes 49200 | solution.py:37
  63.5 4.0 %conditional.11 = (bf16[2,16,128]{2,1,0:T(8,128)(2,1)S(1)}) conditional(s32[]{:T(128)} %bitcast.11, bf16[2,16,128]{2,1,0:T(8,128)(2,1)S(1)} %get-tuple-element.220, bf16[2,16,128]{2,1,0:T(8,128)(2,1)S(1)} %get-tuple-element.220, bf16[2,16,128]{2,1,0:T(8,128)(2,1)S(1)} %get-tuple-element.220, ...), branch_computations={%region_15.16_spmd, %region_16.17_spmd, %region_17.18_spmd, %regio... | conditional | bytes 49200 | solution.py:37
  63.5 2.7 %collective-permute-start.10 = (bf16[2,16,128]{2,1,0:T(8,128)(2,1)S(1)}, bf16[2,16,128]{2,1,0:T(8,128)(2,1)S(1)}, u32[]{:S(2)}, u32[]{:S(2)}) collective-permute-start(bf16[2,16,128]{2,1,0:T(8,128)(2,1)S(1)} %param.14), channel_id=1, source_target_pairs={{0,4},{1,5},{2,6},{3,7},{4,0},{5,1},{6,2},{7,3},{8,12},{9,13},{10,... | collective-permute-start | bytes 24584 | tf_op jit(solution)/shard_map/cond/branch_2_fun/ppermute | solution.py:24
  70.4 12.5 %all_to_all.36 = f32[8,8,1024]{2,1,0:T(8,128)} all-to-all(f32[8,8,1024]{2,1,0:T(8,128)S(1)} %get-tuple-element.162), channel_id=1, replica_groups=mesh['row'=8,'col'=32] {'row'}, dimensions={0} | all-to-all | bytes 524288 | tf_op jit(solution)/shard_map/all_to_all | solution.py:260
  85.2 3.4 %collective-permute-start.31 = (f32[8,128]{1,0:T(8,128)S(1)}, f32[8,128]{1,0:T(8,128)S(1)}, u32[]{:S(2)}, u32[]{:S(2)}) collective-permute-start(f32[8,128]{1,0:T(8,128)S(1)} %fusion.19), channel_id=1, source_target_pairs={{0,1},{1,0},{2,3},{3,2},{4,5},{5,4},{6,7},{7,6},{8,9},{9,8},{10,11... | collective-permute-start | bytes 12296 | tf_op jit(solution)/shard_map/ppermute | solution.py:24
  91.9 3.8 %conditional.13 = (bf16[3,16,128]{2,1,0:T(8,128)(2,1)S(1)}) conditional(s32[]{:T(128)} %bitcast.9, bf16[3,16,128]{2,1,0:T(8,128)(2,1)S(1)} %get-tuple-element.222, bf16[3,16,128]{2,1,0:T(8,128)(2,1)S(1)} %get-tuple-element.222, bf16[3,16,128]{2,1,0:T(8,128)(2,1)S(1)} %get-tuple-element.222, ...), branch_computations={%region_24.25_spmd, %region_25.26_spmd, %region_26.27_spmd, %regio... | conditional | bytes 73776 | solution.py:37
  98.7 13.4 %all_to_all.37 = f32[8,8,1024]{2,1,0:T(8,128)} all-to-all(f32[8,8,1024]{2,1,0:T(8,128)S(1)} %get-tuple-element.172), channel_id=1, replica_groups=mesh['row'=8,'col'=32] {'row'}, dimensions={0} | all-to-all | bytes 524288 | tf_op jit(solution)/shard_map/all_to_all | solution.py:260
  114.3 2.5 %collective-permute-start.32 = (f32[8,128]{1,0:T(8,128)S(1)}, f32[8,128]{1,0:T(8,128)S(1)}, u32[]{:S(2)}, u32[]{:S(2)}) collective-permute-start(f32[8,128]{1,0:T(8,128)S(1)} %fusion.20), channel_id=1, source_target_pairs={{0,1},{1,0},{2,3},{3,2},{4,5},{5,4},{6,7},{7,6},{8,9},{9,8},{10,11... | collective-permute-start | bytes 12296 | tf_op jit(solution)/shard_map/ppermute | solution.py:24
  119.6 4.2 %conditional.14 = (bf16[4,16,128]{2,1,0:T(8,128)(2,1)S(1)}) conditional(s32[]{:T(128)} %bitcast.8, bf16[4,16,128]{2,1,0:T(8,128)(2,1)S(1)} %pad_maximum_fusion.1, bf16[4,16,128]{2,1,0:T(8,128)(2,1)S(1)} %pad_maximum_fusion.1, bf16[4,16,128]{2,1,0:T(8,128)(2,1)S(1)} %pad_maximum_fusion.1, ...), branch_computations={%region_29.30_spmd, %region_30.31_spmd, %region_31.32_spmd, %regio... | conditional | bytes 98352 | solution.py:37
  119.6 3.0 %collective-permute-start.19 = (bf16[4,16,128]{2,1,0:T(8,128)(2,1)S(1)}, bf16[4,16,128]{2,1,0:T(8,128)(2,1)S(1)}, u32[]{:S(2)}, u32[]{:S(2)}) collective-permute-start(bf16[4,16,128]{2,1,0:T(8,128)(2,1)S(1)} %param.26), channel_id=1, source_target_pairs={{0,16},{1,17},{2,18},{3,19},{4,20},{5,21},{6,22},{7,23},{8,24},{9,... | collective-permute-start | bytes 49160 | tf_op jit(solution)/shard_map/cond/branch_2_fun/ppermute | solution.py:24
  123.8 2.6 %conditional.15 = (bf16[4,16,128]{2,1,0:T(8,128)(2,1)S(1)}) conditional(s32[]{:T(128)} %bitcast.7, bf16[4,16,128]{2,1,0:T(8,128)(2,1)S(1)} %get-tuple-element.224, bf16[4,16,128]{2,1,0:T(8,128)(2,1)S(1)} %get-tuple-element.224, bf16[4,16,128]{2,1,0:T(8,128)(2,1)S(1)} %get-tuple-element.224, ...), branch_computations={%region_33.34_spmd, %region_34.35_spmd, %region_35.36_spmd, %regio... | conditional | bytes 98352 | solution.py:37
  123.8 2.6 %collective-permute-done.21 = bf16[4,16,128]{2,1,0:T(8,128)(2,1)S(1)} collective-permute-done((bf16[4,16,128]{2,1,0:T(8,128)(2,1)S(1)}, bf16[4,16,128]{2,1,0:T(8,128)(2,1)S(1)}, u32[]{:S(2)}, u32[]{:S(2)}) %collective-permute-start.21) | collective-permute-done | bytes 16416 | tf_op jit(solution)/shard_map/cond/branch_1_fun/ppermute | solution.py:24
  128.1 12.0 %all_to_all.38 = f32[8,8,1024]{2,1,0:T(8,128)S(1)} all-to-all(f32[8,8,1024]{2,1,0:T(8,128)S(1)} %get-tuple-element.182), channel_id=1, replica_groups=mesh['row'=8,'col'=32] {'row'}, dimensions={0} | all-to-all | bytes 524288 | tf_op jit(solution)/shard_map/all_to_all | solution.py:260
  141.4 3.4 %collective-permute-start.33 = (f32[8,128]{1,0:T(8,128)S(1)}, f32[8,128]{1,0:T(8,128)S(1)}, u32[]{:S(2)}, u32[]{:S(2)}) collective-permute-start(f32[8,128]{1,0:T(8,128)S(1)} %fusion.21), channel_id=1, source_target_pairs={{0,1},{1,0},{2,3},{3,2},{4,5},{5,4},{6,7},{7,6},{8,9},{9,8},{10,11... | collective-permute-start | bytes 12296 | tf_op jit(solution)/shard_map/ppermute | solution.py:24
  146.4 15.1 %all_to_all.39.sent_ref = bf16[16,5,16,128]{3,2,1,0:T(8,128)(2,1)S(1)} all-to-all(bf16[16,5,16,128]{3,2,1,0:T(8,128)(2,1)S(1)} %broadcast_in_dim.198), channel_id=1, replica_groups={{0,2,4,6,8,10,12,14,16,18,20,22,24,26,28,30},{1,3,5,7,9,11,13,15,17,19,..., dimensions={0} | all-to-all | bytes 655360 | tf_op jit(solution)/shard_map/all_to_all | solution.py:19
  164.1 2.8 %shard_map.60 = f32[8,4,16,128]{3,2,1,0:T(8,128)S(1)} custom-call(s32[13]{0:T(128)S(1)} %concatenate.195.at_ref, bf16[16,5,16,128]{3,2,1,0:T(8,128)(2,1)S(1)} %all_to_all.39.sent_ref, bf16[5,4096,128]{2,1,0:T(8,128)(2,1)S(1)} %bitcast.66), custom_call_target="tpu_custom_call" | custom-call | flops 83886080 | bytes 5242880 | tf_op jit(solution)/shard_map/pallas_call | solution.py:173
  166.8 12.6 %all_to_all.40 = f32[8,4,16,128]{3,2,1,0:T(8,128)S(1)} all-to-all(f32[8,4,16,128]{3,2,1,0:T(8,128)S(1)} %shard_map.60), channel_id=1, replica_groups=mesh['row'=8,'col'=32] {'row'}, dimensions={0} | all-to-all | bytes 524288 | tf_op jit(solution)/shard_map/all_to_all | solution.py:282
  (106 shorter events, 54.9 us)
Async XLA Ops:
  0.0 14.4 %copy-start.10 = (s32[16]{0:T(128)S(1)}, s32[16]{0:T(128)}, u32[]{:S(2)}) copy-start(s32[16]{0:T(128)} %param.41) | copy-start | bytes 196
  2.3 12.3 %collective-permute-start.24 = (f32[5,16,128]{2,1,0:T(8,128)S(1)}, f32[5,16,128]{2,1,0:T(8,128)S(1)}, u32[]{:S(2)}, u32[]{:S(2)}) collective-permute-start(f32[5,16,128]{2,1,0:T(8,128)S(1)} %select_reduce_fusion.own_side), channel_id=1, source_target_pairs={{0,1},{1,0},{2,3},{3,2},{4,5},{5,4},{6,7},{7,6},{8,9},{9,8},{10,11... | collective-permute-start | bytes 122888 | tf_op jit(solution)/shard_map/ppermute | solution.py:24
  6.7 1.3 copy-start
  8.1 2.5 %copy-start.2 = (bf16[4096,5,128]{2,0,1:T(8,128)(2,1)S(1)}, bf16[4096,5,128]{2,0,1:T(8,128)(2,1)}, u32[]{:S(2)}) copy-start(bf16[4096,5,128]{2,0,1:T(8,128)(2,1)} %param.37) | copy-start | bytes 15728644
  10.6 27.0 %copy-start.1 = (bf16[5,128,1024]{2,1,0:T(8,128)(2,1)S(1)}, bf16[5,128,1024]{2,1,0:T(8,128)(2,1)}, u32[]{:S(2)}) copy-start(bf16[5,128,1024]{2,1,0:T(8,128)(2,1)} %diag_ref.9) | copy-start | bytes 3932164
  12.6 0.7 copy-start.4
  13.3 15.2 %collective-permute-start.25 = (bf16[1,1024,128]{2,1,0:T(8,128)(2,1)}, bf16[1,1024,128]{2,1,0:T(8,128)(2,1)}, u32[]{:S(2)}, u32[]{:S(2)}) collective-permute-start(bf16[1,1024,128]{2,1,0:T(8,128)(2,1)} %get-tuple-element.144.own_ref), channel_id=1, source_target_pairs={{0,1},{1,0},{2,3},{3,2},{4,5},{5,4},{6,7},{7,6},{8,9},{9,8},{10,11... | collective-permute-start | bytes 786440 | tf_op jit(solution)/shard_map/ppermute | solution.py:24
  13.4 15.2 %collective-permute-start.26 = (bf16[2,1024,128]{2,1,0:T(8,128)(2,1)}, bf16[2,1024,128]{2,1,0:T(8,128)(2,1)}, u32[]{:S(2)}, u32[]{:S(2)}) collective-permute-start(bf16[2,1024,128]{2,1,0:T(8,128)(2,1)} %get-tuple-element.156.own_ref), channel_id=1, source_target_pairs={{0,1},{1,0},{2,3},{3,2},{4,5},{5,4},{6,7},{7,6},{8,9},{9,8},{10,11... | collective-permute-start | bytes 1572872 | tf_op jit(solution)/shard_map/ppermute | solution.py:24
  13.8 14.7 %collective-permute-start.27 = (bf16[3,1024,128]{2,1,0:T(8,128)(2,1)}, bf16[3,1024,128]{2,1,0:T(8,128)(2,1)}, u32[]{:S(2)}, u32[]{:S(2)}) collective-permute-start(bf16[3,1024,128]{2,1,0:T(8,128)(2,1)} %get-tuple-element.166.own_ref), channel_id=1, source_target_pairs={{0,1},{1,0},{2,3},{3,2},{4,5},{5,4},{6,7},{7,6},{8,9},{9,8},{10,11... | collective-permute-start | bytes 2359304 | tf_op jit(solution)/shard_map/ppermute | solution.py:24
  13.9 14.7 %collective-permute-start.28 = (bf16[4,1024,128]{2,1,0:T(8,128)(2,1)S(1)}, bf16[4,1024,128]{2,1,0:T(8,128)(2,1)S(1)}, u32[]{:S(2)}, u32[]{:S(2)}) collective-permute-start(bf16[4,1024,128]{2,1,0:T(8,128)(2,1)S(1)} %get-tuple-element.176.own_ref), channel_id=1, source_target_pairs={{0,1},{1,0},{2,3},{3,2},{4,5},{5,4},{6,7},{7,6},{8,9},{9,8},{10,11... | collective-permute-start | bytes 3145736 | tf_op jit(solution)/shard_map/ppermute | solution.py:24
  15.2 13.4 %all-to-all-start = ((f32[8,8,128]{2,1,0:T(8,128)}), f32[8,8,128]{2,1,0:T(8,128)S(1)}, u32[]{:S(2)}, u32[]{:S(2)}) async-start(f32[8,8,128]{2,1,0:T(8,128)} %broadcast_in_dim.172), calls=%async_computation | async-start | bytes 65536 | tf_op jit(solution)/shard_map/all_to_all | solution.py:19
  30.4 2.3 %collective-permute-start.29 = (f32[8,128]{1,0:T(8,128)S(1)}, f32[8,128]{1,0:T(8,128)S(1)}, u32[]{:S(2)}, u32[]{:S(2)}) collective-permute-start(f32[8,128]{1,0:T(8,128)S(1)} %fusion), channel_id=1, source_target_pairs={{0,1},{1,0},{2,3},{3,2},{4,5},{5,4},{6,7},{7,6},{8,9},{9,8},{10,11... | collective-permute-start | bytes 12296 | tf_op jit(solution)/shard_map/ppermute | solution.py:24
  33.5 4.0 %collective-permute-start.1 = (bf16[1,16,128]{2,1,0:T(8,128)(2,1)S(1)}, bf16[1,16,128]{2,1,0:T(8,128)(2,1)S(1)}, u32[]{:S(2)}, u32[]{:S(2)}) collective-permute-start(bf16[1,16,128]{2,1,0:T(8,128)(2,1)S(1)} %param.2), channel_id=1, source_target_pairs={{0,16},{1,17},{2,18},{3,19},{4,20},{5,21},{6,22},{7,23},{8,24},{9,... | collective-permute-start | bytes 12296 | tf_op jit(solution)/shard_map/cond/branch_2_fun/ppermute | solution.py:24
  55.5 3.9 %collective-permute-start.30 = (f32[8,128]{1,0:T(8,128)S(1)}, f32[8,128]{1,0:T(8,128)S(1)}, u32[]{:S(2)}, u32[]{:S(2)}) collective-permute-start(f32[8,128]{1,0:T(8,128)S(1)} %fusion.18), channel_id=1, source_target_pairs={{0,1},{1,0},{2,3},{3,2},{4,5},{5,4},{6,7},{7,6},{8,9},{9,8},{10,11... | collective-permute-start | bytes 12296 | tf_op jit(solution)/shard_map/ppermute | solution.py:24
  61.0 2.5 %collective-permute-start.6 = (bf16[2,16,128]{2,1,0:T(8,128)(2,1)S(1)}, bf16[2,16,128]{2,1,0:T(8,128)(2,1)S(1)}, u32[]{:S(2)}, u32[]{:S(2)}) collective-permute-start(bf16[2,16,128]{2,1,0:T(8,128)(2,1)S(1)} %param.9), channel_id=1, source_target_pairs={{0,8},{1,9},{2,10},{3,11},{4,12},{5,13},{6,14},{7,15},{8,0},{9,1},... | collective-permute-start | bytes 24584 | tf_op jit(solution)/shard_map/cond/branch_1_fun/ppermute | solution.py:24
  63.5 4.0 %collective-permute-start.10 = (bf16[2,16,128]{2,1,0:T(8,128)(2,1)S(1)}, bf16[2,16,128]{2,1,0:T(8,128)(2,1)S(1)}, u32[]{:S(2)}, u32[]{:S(2)}) collective-permute-start(bf16[2,16,128]{2,1,0:T(8,128)(2,1)S(1)} %param.14), channel_id=1, source_target_pairs={{0,4},{1,5},{2,6},{3,7},{4,0},{5,1},{6,2},{7,3},{8,12},{9,13},{10,... | collective-permute-start | bytes 24584 | tf_op jit(solution)/shard_map/cond/branch_2_fun/ppermute | solution.py:24
  85.2 4.5 %collective-permute-start.31 = (f32[8,128]{1,0:T(8,128)S(1)}, f32[8,128]{1,0:T(8,128)S(1)}, u32[]{:S(2)}, u32[]{:S(2)}) collective-permute-start(f32[8,128]{1,0:T(8,128)S(1)} %fusion.19), channel_id=1, source_target_pairs={{0,1},{1,0},{2,3},{3,2},{4,5},{5,4},{6,7},{7,6},{8,9},{9,8},{10,11... | collective-permute-start | bytes 12296 | tf_op jit(solution)/shard_map/ppermute | solution.py:24
  91.9 3.8 %collective-permute-start.17 = (bf16[3,16,128]{2,1,0:T(8,128)(2,1)S(1)}, bf16[3,16,128]{2,1,0:T(8,128)(2,1)S(1)}, u32[]{:S(2)}, u32[]{:S(2)}) collective-permute-start(bf16[3,16,128]{2,1,0:T(8,128)(2,1)S(1)} %param.23), channel_id=1, source_target_pairs={{0,6},{1,7},{2,4},{3,5},{4,2},{5,3},{6,0},{7,1},{8,14},{9,15},{10,... | collective-permute-start | bytes 36872 | tf_op jit(solution)/shard_map/cond/branch_3_fun/ppermute | solution.py:24
  114.3 3.7 %collective-permute-start.32 = (f32[8,128]{1,0:T(8,128)S(1)}, f32[8,128]{1,0:T(8,128)S(1)}, u32[]{:S(2)}, u32[]{:S(2)}) collective-permute-start(f32[8,128]{1,0:T(8,128)S(1)} %fusion.20), channel_id=1, source_target_pairs={{0,1},{1,0},{2,3},{3,2},{4,5},{5,4},{6,7},{7,6},{8,9},{9,8},{10,11... | collective-permute-start | bytes 12296 | tf_op jit(solution)/shard_map/ppermute | solution.py:24
  119.6 4.2 %collective-permute-start.19 = (bf16[4,16,128]{2,1,0:T(8,128)(2,1)S(1)}, bf16[4,16,128]{2,1,0:T(8,128)(2,1)S(1)}, u32[]{:S(2)}, u32[]{:S(2)}) collective-permute-start(bf16[4,16,128]{2,1,0:T(8,128)(2,1)S(1)} %param.26), channel_id=1, source_target_pairs={{0,16},{1,17},{2,18},{3,19},{4,20},{5,21},{6,22},{7,23},{8,24},{9,... | collective-permute-start | bytes 49160 | tf_op jit(solution)/shard_map/cond/branch_2_fun/ppermute | solution.py:24
  123.8 2.6 %collective-permute-start.21 = (bf16[4,16,128]{2,1,0:T(8,128)(2,1)S(1)}, bf16[4,16,128]{2,1,0:T(8,128)(2,1)S(1)}, u32[]{:S(2)}, u32[]{:S(2)}) collective-permute-start(bf16[4,16,128]{2,1,0:T(8,128)(2,1)S(1)} %param.29), channel_id=1, source_target_pairs={{0,2},{1,3},{2,0},{3,1},{4,6},{5,7},{6,4},{7,5},{8,10},{9,11},{10,... | collective-permute-start | bytes 49160 | tf_op jit(solution)/shard_map/cond/branch_1_fun/ppermute | solution.py:24
  128.1 51.3 %copy-start.9 = (f32[16,4,128]{2,1,0:T(4,128)S(1)}, f32[16,4,128]{2,1,0:T(4,128)}, u32[]{:S(2)}) copy-start(f32[16,4,128]{2,1,0:T(4,128)} %param.39) | copy-start | bytes 98308
  141.4 4.2 %collective-permute-start.33 = (f32[8,128]{1,0:T(8,128)S(1)}, f32[8,128]{1,0:T(8,128)S(1)}, u32[]{:S(2)}, u32[]{:S(2)}) collective-permute-start(f32[8,128]{1,0:T(8,128)S(1)} %fusion.21), channel_id=1, source_target_pairs={{0,1},{1,0},{2,3},{3,2},{4,5},{5,4},{6,7},{7,6},{8,9},{9,8},{10,11... | collective-permute-start | bytes 12296 | tf_op jit(solution)/shard_map/ppermute | solution.py:24
  161.6 2.5 %copy-start.3 = (bf16[4096,5,128]{2,0,1:T(8,128)(2,1)S(1)}, bf16[4096,5,128]{2,0,1:T(8,128)(2,1)}, u32[]{:S(2)}) copy-start(bf16[4096,5,128]{2,0,1:T(8,128)(2,1)} %param.37) | copy-start | bytes 15728644
  (4 other events, 2.9 us)
